TPU v7x, 32 devices: a whole 2x2x4 slice. The times are simulated.
32 devices in a mesh: dp: 1, sp: 32 (over x, y, z, core).
Axes of the slice: x: 2, y: 2, z: 4, core: 2. Of those that a mesh axis runs over, the one named last changes fastest.
Arguments:
- q: bfloat16 [32, 8, 256], P('dp')
- k: bfloat16 [32, 8192, 8, 256], P('dp', 'sp')
- v: bfloat16 [32, 8192, 8, 256], P('dp', 'sp')
Outputs:
- q: bfloat16 [32, 8, 256], P('dp')
All inputs are finite; a program needn't handle non-finite values.
Results may differ from a plain program's by a relative error of at most 0.012.
Values are sent between devices in bfloat16 or wider.
A program may use at most 2 GiB of HBM per device.

v0:
```python
import jax
import jax.numpy as jnp
from jax import lax
from jax.sharding import PartitionSpec as P


def einsum(form, a, b):
    return jnp.einsum(form, a.astype(jnp.float32), b.astype(jnp.float32))


def part_of(q, k, v):
    grouped = q.reshape(q.shape[0], k.shape[2], -1, q.shape[2])
    scores = einsum("bgsd,bugd->bgsu", grouped, k) * q.shape[2] ** -0.5
    high = jnp.max(scores, -1, keepdims=True)
    weights = jnp.exp(scores - high)
    seen = einsum("bgsu,bugd->bgsd", weights.astype(jnp.bfloat16), v)
    return jnp.concatenate([seen, jnp.sum(weights, -1, keepdims=True), high], -1)


def together(parts):
    seen, total, high = parts[..., :-2], parts[..., -2:-1], parts[..., -1:]
    scale = jnp.exp(high - jnp.max(high, 0))
    return (jnp.sum(seen * scale, 0) / jnp.sum(total * scale, 0)).astype(jnp.bfloat16)


def solution(mesh):
    def step(q, k, v):
        return together(lax.all_gather(part_of(q, k, v), "sp")).reshape(q.shape)

    return jax.shard_map(
        step,
        mesh=mesh,
        in_specs=(P("dp", None, None), P("dp", "sp", None, None), P("dp", "sp", None, None)),
        out_specs=P("dp", None, None),
        check_vma=False,
    )
```

profile of v0, /device:TPU:0, one launch (start us, length us, event | category | flops | bytes accessed | tf_op | source)
XLA Modules:
  0.0 174.5 jit_solution(10047620140047485205)
XLA Ops:
  6.5 0.0 all-gather.3.cloned.1.call-start
  6.5 18.1 %fusion.2 = f32[32,8,1,256]{3,2,1,0:T(1,128)S(1)} fusion(bf16[32,256,8,256]{3,2,1,0:T(8,128)(2,1)} %param.4, bf16[32,8,256,1]{2,1,0,3:T(8,128)(2,1)} %bitcast.27), kind=kOutput, calls=%fused_computation.2 | convolution fusion | flops 33554432 | bytes 33947648 | tf_op jit(solution)/shard_map/bgsd,bugd->bgsu/dot_general | solution.py:8
  24.6 0.1 fusion.10
  24.7 0.2 fusion.11
  24.9 0.3 copy.23
  25.2 0.3 copy.22
  25.5 19.1 %fusion = f32[32,8,1,256]{3,2,1,0:T(1,128)S(1)} fusion(bf16[32,256,8,256]{3,2,1,0:T(8,128)(2,1)} %param.5, bf16[32,8,256,1]{2,1,0,3:T(8,128)(2,1)S(1)} %get-tuple-element.7), kind=kOutput, calls=%fused_computation | convolution fusion | flops 33554432 | bytes 33947648 | tf_op jit(solution)/shard_map/bgsu,bugd->bgsd/dot_general | solution.py:8
  44.6 0.9 pad_maximum_fusion
  45.5 0.0 all-gather.3.cloned.1.call-update
  45.5 98.9 %all-gather.3.cloned.1.call-done = f32[1024,8,1,258]{3,1,2,0:T(8,128)} async-done(((f32[32,8,1,258]{3,1,2,0:T(8,128)}), f32[1024,8,1,258]{3,1,2,0:T(8,128)}) %all-gather.3.cloned.1.call-update) | async-done | bytes 8454160 | tf_op jit(solution)/shard_map/all_gather | solution.py:28
  144.4 3.5 %slice_reduce_fusion = f32[32,8]{1,0:T(8,128)S(1)} fusion(f32[32,32,8,1,258]{4,2,1,0,3:T(8,128)} %bitcast.22), kind=kLoop, calls=%fused_computation.9 | loop fusion | flops 7936 | bytes 33792 | tf_op jit(solution)/shard_map/reduce_max | solution.py:22
  147.9 7.1 %fusion.5 = (f32[32,8]{1,0:T(8,128)S(1)}, f32[32,32,8,1,1]{4,2,1,0,3:T(8,128)}) fusion(f32[32,32,8,1,258]{4,2,1,0,3:T(8,128)} %bitcast.23, f32[32,8]{1,0:T(8,128)S(1)} %slice_reduce_fusion), kind=kLoop, calls=%fused_computation.7 | loop fusion | flops 24320 | bytes 100352 | tf_op jit(solution)/shard_map/reduce_sum | solution.py:23
  155.0 7.7 %copy.36 = f32[32,32,8,1,1]{2,1,0,3,4:T(8,128)S(1)} copy(f32[32,32,8,1,1]{4,2,1,0,3:T(8,128)} %get-tuple-element.6) | data formatting | bytes 65536 | tf_op jit(solution)/shard_map/mul | solution.py:23
  162.7 4.2 %fusion.4 = f32[32,8,256]{2,1,0:T(8,128)S(1)} fusion(f32[32,32,8,1,258]{4,2,1,0,3:T(8,128)} %bitcast.24, f32[32,32,8]{2,1,0:T(8,128)S(1)} %bitcast.25), kind=kLoop, calls=%fused_computation.5 | loop fusion | flops 4128768 | bytes 8683520 | tf_op jit(solution)/shard_map/reduce_sum | solution.py:23
  166.9 0.8 divide_convert_fusion
  (1 shorter events, 0.0 us)
Async XLA Ops:
  6.5 137.8 %all-gather.3.cloned.1.call-start = ((), (), s32[]{:S(2)}) async-start(), calls=%async_computation | async-start | bytes 12976128 | tf_op jit(solution)/shard_map/all_gather | solution.py:28
Sparse Core Ops, SparseCore 0:
  45.6 98.7 all-gather.2
where the time goes:
time: 175 us
  waiting for transfers between devices  98.9 us (57%)
  matrix products  37.2 us (21%)
  other arithmetic  16.8 us (10%)
  between operations  13.4 us (8%)
  local copies, waits for them, and re-layouts  8.21 us (5%)
    all_gather x1, waiting for transfers between devices, step(): return together(lax.all_gather(part_of(q, k, v), 'sp')).reshape(q.shape)  98.9 us
    dot_general x2, matrix products, einsum(): return jnp.einsum(form, a.astype(jnp.float32), b.astype(jnp.float32))  37.2 us
    mul x1, local copies, waits for them, and re-layouts, together(): seen * scale  7.67 us
    reduce_sum x1, other arithmetic, together(): jnp.sum(total * scale, 0)  7.13 us
    reduce_sum x1, other arithmetic, together(): jnp.sum(seen * scale, 0) / jnp.sum(total * scale, 0)  4.22 us
    reduce_max x1, other arithmetic, together(): scale = jnp.exp(high - jnp.max(high, 0))  3.52 us
  transfers between devices with their start and end apart: 1, of which 1 were waited for; matrix products, arithmetic and copies ran while one was open for 0% of the time, Pallas kernels for 0%

commit v1 on v0

v1 whole, which is shorter than its diff:
```python
import functools

import jax
import jax.numpy as jnp
from jax import lax
from jax.experimental import pallas as pl
from jax.experimental.pallas import tpu as pltpu
from jax.sharding import PartitionSpec as P

SLOTS = 8
LAG = 6


def flip(index, mask, bits):
    out = 0
    for bit in range(bits):
        a, b = index // 2**bit % 2, mask // 2**bit % 2
        out = out + 2**bit * (a + b - 2 * a * b)
    return out


def kernel(n, bits, q_hbm, k_hbm, v_hbm, out, q, k, v, seen, stats, seen_in, stats_in, q_sem, k_sem, v_sem, send_sem, recv_sem, out_send, out_recv):
    me = lax.axis_index("sp")
    seqs = q.shape[0]

    def owner(step):
        return flip(me, n - 1 - step, bits)

    def load(hbm, buf, sem, step):
        slot = lax.rem(step, SLOTS)
        return pltpu.make_async_copy(hbm.at[owner(step)], buf.at[slot], sem.at[slot])

    q_copy = pltpu.make_async_copy(q_hbm, q, q_sem)
    q_copy.start()

    @pl.loop(0, SLOTS)
    def _(step):
        load(k_hbm, k, k_sem, step).start()
        load(v_hbm, v, v_sem, step).start()

    barrier = pltpu.get_barrier_semaphore()

    @pl.loop(1, n)
    def _(hop):
        pl.semaphore_signal(barrier, inc=1, device_id={"sp": lax.rem(me + hop, n)}, device_id_type=pl.DeviceIdType.MESH)

    q_copy.wait()

    heads, head = q.shape[1:]
    lane = lax.broadcasted_iota(jnp.int32, (heads, k.shape[1] * heads), 1)
    own = lane % heads == lax.broadcasted_iota(jnp.int32, lane.shape, 0)

    def scores(step):
        load(k_hbm, k, k_sem, step).wait()
        keys = k[lax.rem(step, SLOTS)].reshape(-1, head)
        s = lax.dot_general(q[owner(step)], keys, (((1,), (1,)), ((), ())), preferred_element_type=jnp.float32) * head**-0.5
        s = jnp.where(own, s, -jnp.inf)
        high = jnp.max(s, -1, keepdims=True)
        w = jnp.exp(s - high)
        return w.astype(jnp.bfloat16), high, jnp.sum(w, -1, keepdims=True)

    def values(step, w):
        load(v_hbm, v, v_sem, step).wait()
        vals = v[lax.rem(step, SLOTS)].reshape(-1, head)
        return lax.dot_general(w, vals, (((1,), (0,)), ((), ())), preferred_element_type=jnp.float32)

    def keep(step, o, high, total):
        seen[step] = o.astype(jnp.bfloat16)
        stats[step] = jnp.concatenate([jnp.broadcast_to(high, (heads, 128)), jnp.broadcast_to(total, (heads, 128))], -1)

    def send(step):
        to = owner(step)
        args = dict(device_id={"sp": to}, device_id_type=pl.DeviceIdType.MESH)
        return (
            pltpu.make_async_remote_copy(seen.at[step], seen_in.at[step], send_sem.at[0], recv_sem.at[0], **args),
            pltpu.make_async_remote_copy(stats.at[step], stats_in.at[step], send_sem.at[1], recv_sem.at[1], **args),
        )

    def body(step, carry):
        w, high, total = carry
        new = scores(step)
        o = values(step - 1, w)
        keep(step - 1, o, high, total)

        @pl.when(step + SLOTS < n)
        def _():
            load(k_hbm, k, k_sem, step + SLOTS).start()

        @pl.when(step - 1 + SLOTS < n)
        def _():
            load(v_hbm, v, v_sem, step - 1 + SLOTS).start()

        @pl.when(step == LAG)
        def _():
            pl.semaphore_wait(barrier, n - 1)

            @pl.loop(0, LAG - 1)
            def _(earlier):
                for copy in send(earlier):
                    copy.start()

        @pl.when(step >= LAG)
        def _():
            for copy in send(step - 1):
                copy.start()

        return new

    first = scores(0)

    @pl.when(SLOTS < n)
    def _():
        load(k_hbm, k, k_sem, SLOTS).start()

    w, high, total = lax.fori_loop(1, n, body, first)
    o = values(n - 1, w)

    pltpu.make_async_copy(seen_in.at[pl.ds(0, n - 1)], seen_in.at[pl.ds(0, n - 1)], recv_sem.at[0]).wait()
    pltpu.make_async_copy(stats_in.at[pl.ds(0, n - 1)], stats_in.at[pl.ds(0, n - 1)], recv_sem.at[1]).wait()
    highs = [stats_in[i, :, :128] for i in range(n - 1)] + [jnp.broadcast_to(high, (heads, 128))]
    totals = [stats_in[i, :, 128:] for i in range(n - 1)] + [jnp.broadcast_to(total, (heads, 128))]
    parts = [seen_in[i] for i in range(n - 1)] + [o]
    top = functools.reduce(jnp.maximum, highs)
    scale = [jnp.exp(x - top) for x in highs]
    bottom = functools.reduce(jnp.add, [x * y for x, y in zip(scale, totals)])
    wide = lambda x: jnp.concatenate([x] * (head // 128), -1)
    upper = functools.reduce(jnp.add, [wide(x) * y.astype(jnp.float32) for x, y in zip(scale, parts)])
    out[me] = (upper / wide(bottom)).astype(jnp.bfloat16)

    def result(hop):
        return pltpu.make_async_remote_copy(out.at[me], out.at[me], out_send, out_recv, device_id={"sp": flip(me, hop, bits)}, device_id_type=pl.DeviceIdType.MESH)

    @pl.loop(0, n - 1)
    def _(hop):
        result(n - 1 - hop).start()

    pltpu.make_async_copy(seen.at[pl.ds(0, n - 1)], seen.at[pl.ds(0, n - 1)], send_sem.at[0]).wait()
    pltpu.make_async_copy(stats.at[pl.ds(0, n - 1)], stats.at[pl.ds(0, n - 1)], send_sem.at[1]).wait()
    pltpu.make_async_copy(out.at[pl.ds(0, n - 1)], out.at[pl.ds(0, n - 1)], out_send).wait()
    pltpu.make_async_copy(out.at[pl.ds(0, n - 1)], out.at[pl.ds(0, n - 1)], out_recv).wait()


def solution(mesh):
    n = mesh.shape["sp"]

    def step(q, k, v):
        seqs, tokens, heads, head = k.shape
        return pl.pallas_call(
            functools.partial(kernel, n, (n - 1).bit_length()),
            out_shape=jax.ShapeDtypeStruct(q.shape, q.dtype),
            in_specs=[pl.BlockSpec(memory_space=pl.ANY)] * 3,
            out_specs=pl.BlockSpec(memory_space=pltpu.VMEM),
            scratch_shapes=[
                pltpu.VMEM(q.shape, q.dtype),
                pltpu.VMEM((SLOTS, tokens, heads, head), k.dtype),
                pltpu.VMEM((SLOTS, tokens, heads, head), v.dtype),
                pltpu.VMEM((n, heads, head), jnp.bfloat16),
                pltpu.VMEM((n, heads, 256), jnp.float32),
                pltpu.VMEM((n, heads, head), jnp.bfloat16),
                pltpu.VMEM((n, heads, 256), jnp.float32),
                pltpu.SemaphoreType.DMA,
                pltpu.SemaphoreType.DMA((SLOTS,)),
                pltpu.SemaphoreType.DMA((SLOTS,)),
                pltpu.SemaphoreType.DMA((2,)),
                pltpu.SemaphoreType.DMA((2,)),
                pltpu.SemaphoreType.DMA,
                pltpu.SemaphoreType.DMA,
            ],
            compiler_params=pltpu.CompilerParams(collective_id=0, has_side_effects=True, vmem_limit_bytes=60 * 2**20),
        )(q, k, v)

    return jax.shard_map(
        step,
        mesh=mesh,
        in_specs=(P("dp", None, None), P("dp", "sp", None, None), P("dp", "sp", None, None)),
        out_specs=P("dp", None, None),
        check_vma=False,
    )
```

time: 175 us -> 49 us (0.28)
  waiting for transfers between devices: 98.9 us -> 0 us
  Pallas kernels: 0 us -> 47.2 us
  matrix products: 37.2 us -> 0 us
  other arithmetic: 16.8 us -> 0 us
  between operations: 13.4 us -> 0.01 us
  local copies, waits for them, and re-layouts: 8.21 us -> 1.57 us
    all_gather x1 -> x0, waiting for transfers between devices: 98.9 us -> none  [step(): return together(lax.all_gather(part_of(q, k, v), 'sp')).reshape(q.shape)]
    pallas_call x0 -> x1, Pallas kernels: none -> 47.2 us  [step(): pl.pallas_call(functools.partial(kernel, n, (n - 1).bit_length()), out_sh...]
    dot_general x2 -> x0, matrix products: 37.2 us -> none  [einsum(): return jnp.einsum(form, a.astype(jnp.float32), b.astype(jnp.float32))]
    reduce_sum x2 -> x0, other arithmetic: 11.4 us -> none  [the longest x1 7.13 us: together(): jnp.sum(total * scale, 0)]
    mul x1 -> x0, local copies, waits for them, and re-layouts: 7.67 us -> none  [together(): seen * scale]
    reduce_max x2 -> x0, other arithmetic: 3.64 us -> none  [the longest x1 3.52 us: together(): scale = jnp.exp(high - jnp.max(high, 0))]
  transfers between devices with their start and end apart: 1 -> 0, of which waited for: 1 -> 0; matrix products, arithmetic and copies ran while one was open for 0% -> 0% of each run, Pallas kernels for 0% -> 0%
where the time goes in v1:
time: 49 us; the launch traced here: 48.8 us
  Pallas kernels  47.2 us (96%)
  local copies, waits for them, and re-layouts  1.57 us (3%)
    pallas_call x1, Pallas kernels, step(): pl.pallas_call(functools.partial(kernel, n, (n - 1).bit_length()), out_sh...  47.2 us
    unnamed x1, local copies, waits for them, and re-layouts  1.57 us

profile of v1, /device:TPU:0, one launch (start us, length us, event | category | flops | bytes accessed | tf_op | source)
XLA Modules:
  0.0 48.8 jit_solution(13354026975318401995)
XLA Ops:
  0.0 47.2 %shard_map.37 = bf16[32,8,256]{2,1,0:T(8,128)(2,1)} custom-call(bf16[32,8,256]{2,1,0:T(8,128)(2,1)} %q_hbm.1, bf16[32,256,8,256]{3,2,1,0:T(8,128)(2,1)} %k_hbm.1, bf16[32,256,8,256]{3,2,1,0:T(8,128)(2,1)} %v_hbm.1), custom_call_target="tpu_custom_call" | custom-call | tf_op jit(solution)/shard_map/pallas_call | solution.py:148
  47.2 1.6 %copy.5 = bf16[32,8,256]{2,1,0:T(8,128)(2,1)} copy(bf16[32,8,256]{2,1,0:T(8,128)(2,1)} %shard_map.37) | data formatting | bytes 262144

commit v2 on v1

--- a/solution.py
+++ b/solution.py
@@ -11,20 +11,12 @@
 LAG = 6
 
 
-def flip(index, mask, bits):
-    out = 0
-    for bit in range(bits):
-        a, b = index // 2**bit % 2, mask // 2**bit % 2
-        out = out + 2**bit * (a + b - 2 * a * b)
-    return out
-
-
-def kernel(n, bits, q_hbm, k_hbm, v_hbm, out, q, k, v, seen, stats, seen_in, stats_in, q_sem, k_sem, v_sem, send_sem, recv_sem, out_send, out_recv):
+def kernel(n, q_hbm, k_hbm, v_hbm, out, q, k, v, raw, weights, seen, stats, seen_in, stats_in, q_sem, k_sem, v_sem, send_sem, recv_sem, out_send, out_recv):
     me = lax.axis_index("sp")
     seqs = q.shape[0]
 
     def owner(step):
-        return flip(me, n - 1 - step, bits)
+        return lax.bitwise_xor(me, n - 1 - step)
 
     def load(hbm, buf, sem, step):
         slot = lax.rem(step, SLOTS)
@@ -51,22 +43,22 @@
     own = lane % heads == lax.broadcasted_iota(jnp.int32, lane.shape, 0)
 
     def scores(step):
-        load(k_hbm, k, k_sem, step).wait()
         keys = k[lax.rem(step, SLOTS)].reshape(-1, head)
-        s = lax.dot_general(q[owner(step)], keys, (((1,), (1,)), ((), ())), preferred_element_type=jnp.float32) * head**-0.5
-        s = jnp.where(own, s, -jnp.inf)
+        return lax.dot_general(q[owner(step)], keys, (((1,), (1,)), ((), ())), preferred_element_type=jnp.float32)
+
+    def soften(step, s):
+        s = jnp.where(own, s * head**-0.5, -jnp.inf)
         high = jnp.max(s, -1, keepdims=True)
         w = jnp.exp(s - high)
-        return w.astype(jnp.bfloat16), high, jnp.sum(w, -1, keepdims=True)
+        total = jnp.sum(w, -1, keepdims=True)
+        stats[step] = jnp.concatenate([jnp.broadcast_to(high, (heads, 128)), jnp.broadcast_to(total, (heads, 128))], -1)
+        return w.astype(jnp.bfloat16)
 
     def values(step, w):
-        load(v_hbm, v, v_sem, step).wait()
         vals = v[lax.rem(step, SLOTS)].reshape(-1, head)
-        return lax.dot_general(w, vals, (((1,), (0,)), ((), ())), preferred_element_type=jnp.float32)
-
-    def keep(step, o, high, total):
-        seen[step] = o.astype(jnp.bfloat16)
-        stats[step] = jnp.concatenate([jnp.broadcast_to(high, (heads, 128)), jnp.broadcast_to(total, (heads, 128))], -1)
+        half = vals.shape[0] // 2
+        dot = lambda a, b: lax.dot_general(a, b, (((1,), (0,)), ((), ())), preferred_element_type=jnp.float32)
+        return dot(w[:, :half], vals[:half]) + dot(w[:, half:], vals[half:])
 
     def send(step):
         to = owner(step)
@@ -76,49 +68,64 @@
             pltpu.make_async_remote_copy(stats.at[step], stats_in.at[step], send_sem.at[1], recv_sem.at[1], **args),
         )
 
-    def body(step, carry):
-        w, high, total = carry
-        new = scores(step)
-        o = values(step - 1, w)
-        keep(step - 1, o, high, total)
+    def wait(hbm, buf, sem, step):
+        load(hbm, buf, sem, step).wait()
 
+    def refill(hbm, buf, sem, step):
         @pl.when(step + SLOTS < n)
         def _():
-            load(k_hbm, k, k_sem, step + SLOTS).start()
+            load(hbm, buf, sem, step + SLOTS).start()
 
-        @pl.when(step - 1 + SLOTS < n)
-        def _():
-            load(v_hbm, v, v_sem, step - 1 + SLOTS).start()
+    wait(k_hbm, k, k_sem, 0)
+    raw[...] = scores(0)
+    refill(k_hbm, k, k_sem, 0)
+    wait(k_hbm, k, k_sem, 1)
+    old = raw[...]
+    raw[...] = scores(1)
+    weights[...] = soften(0, old)
+    refill(k_hbm, k, k_sem, 1)
+
+    @pl.loop(2, n)
+    def _(step):
+        wait(v_hbm, v, v_sem, step - 2)
+        wait(k_hbm, k, k_sem, step)
+        old, w = raw[...], weights[...]
+        new = scores(step)
+        o = values(step - 2, w)
+        weights[...] = soften(step - 1, old)
+        raw[...] = new
+        seen[step - 2] = o.astype(jnp.bfloat16)
+        refill(v_hbm, v, v_sem, step - 2)
+        refill(k_hbm, k, k_sem, step)
 
         @pl.when(step == LAG)
         def _():
             pl.semaphore_wait(barrier, n - 1)
 
-            @pl.loop(0, LAG - 1)
+            @pl.loop(0, LAG - 2)
             def _(earlier):
                 for copy in send(earlier):
                     copy.start()
 
         @pl.when(step >= LAG)
         def _():
-            for copy in send(step - 1):
+            for copy in send(step - 2):
                 copy.start()
 
-        return new
-
-    first = scores(0)
-
-    @pl.when(SLOTS < n)
-    def _():
-        load(k_hbm, k, k_sem, SLOTS).start()
-
-    w, high, total = lax.fori_loop(1, n, body, first)
-    o = values(n - 1, w)
+    w = weights[...]
+    weights[...] = soften(n - 1, raw[...])
+    wait(v_hbm, v, v_sem, n - 2)
+    seen[n - 2] = values(n - 2, w).astype(jnp.bfloat16)
+    for copy in send(n - 2):
+        copy.start()
+    wait(v_hbm, v, v_sem, n - 1)
+    o = values(n - 1, weights[...])
+    high, total = stats[n - 1, :, :128], stats[n - 1, :, 128:]
 
     pltpu.make_async_copy(seen_in.at[pl.ds(0, n - 1)], seen_in.at[pl.ds(0, n - 1)], recv_sem.at[0]).wait()
     pltpu.make_async_copy(stats_in.at[pl.ds(0, n - 1)], stats_in.at[pl.ds(0, n - 1)], recv_sem.at[1]).wait()
-    highs = [stats_in[i, :, :128] for i in range(n - 1)] + [jnp.broadcast_to(high, (heads, 128))]
-    totals = [stats_in[i, :, 128:] for i in range(n - 1)] + [jnp.broadcast_to(total, (heads, 128))]
+    highs = [stats_in[i, :, :128] for i in range(n - 1)] + [high]
+    totals = [stats_in[i, :, 128:] for i in range(n - 1)] + [total]
     parts = [seen_in[i] for i in range(n - 1)] + [o]
     top = functools.reduce(jnp.maximum, highs)
     scale = [jnp.exp(x - top) for x in highs]
@@ -128,7 +135,7 @@
     out[me] = (upper / wide(bottom)).astype(jnp.bfloat16)
 
     def result(hop):
-        return pltpu.make_async_remote_copy(out.at[me], out.at[me], out_send, out_recv, device_id={"sp": flip(me, hop, bits)}, device_id_type=pl.DeviceIdType.MESH)
+        return pltpu.make_async_remote_copy(out.at[me], out.at[me], out_send, out_recv, device_id={"sp": lax.bitwise_xor(me, hop)}, device_id_type=pl.DeviceIdType.MESH)
 
     @pl.loop(0, n - 1)
     def _(hop):
@@ -146,7 +153,7 @@
     def step(q, k, v):
         seqs, tokens, heads, head = k.shape
         return pl.pallas_call(
-            functools.partial(kernel, n, (n - 1).bit_length()),
+            functools.partial(kernel, n),
             out_shape=jax.ShapeDtypeStruct(q.shape, q.dtype),
             in_specs=[pl.BlockSpec(memory_space=pl.ANY)] * 3,
             out_specs=pl.BlockSpec(memory_space=pltpu.VMEM),
@@ -154,6 +161,8 @@
                 pltpu.VMEM(q.shape, q.dtype),
                 pltpu.VMEM((SLOTS, tokens, heads, head), k.dtype),
                 pltpu.VMEM((SLOTS, tokens, heads, head), v.dtype),
+                pltpu.VMEM((heads, tokens * heads), jnp.float32),
+                pltpu.VMEM((heads, tokens * heads), jnp.bfloat16),
                 pltpu.VMEM((n, heads, head), jnp.bfloat16),
                 pltpu.VMEM((n, heads, 256), jnp.float32),
                 pltpu.VMEM((n, heads, head), jnp.bfloat16),

time: 49 us -> 34.4 us (0.70)
  Pallas kernels: 47.2 us -> 32.6 us
    pallas_call x1, Pallas kernels: 47.2 us -> 32.6 us  [step(): pl.pallas_call(functools.partial(kernel, n), out_shape=jax.ShapeDtypeStru...]
where the time goes in v2:
time: 34.4 us; the launch traced here: 34.2 us
  Pallas kernels  32.6 us (95%)
  local copies, waits for them, and re-layouts  1.57 us (5%)
    pallas_call x1, Pallas kernels, step(): pl.pallas_call(functools.partial(kernel, n), out_shape=jax.ShapeDtypeStru...  32.6 us
    unnamed x1, local copies, waits for them, and re-layouts  1.57 us

profile of v2, /device:TPU:0, one launch (start us, length us, event | category | flops | bytes accessed | tf_op | source)
XLA Modules:
  0.0 34.2 jit_solution(5365782968315359688)
XLA Ops:
  0.0 32.6 %shard_map.37 = bf16[32,8,256]{2,1,0:T(8,128)(2,1)} custom-call(bf16[32,8,256]{2,1,0:T(8,128)(2,1)} %q_hbm.1, bf16[32,256,8,256]{3,2,1,0:T(8,128)(2,1)} %k_hbm.1, bf16[32,256,8,256]{3,2,1,0:T(8,128)(2,1)} %v_hbm.1), custom_call_target="tpu_custom_call" | custom-call | tf_op jit(solution)/shard_map/pallas_call | solution.py:155
  32.6 1.6 %copy.5 = bf16[32,8,256]{2,1,0:T(8,128)(2,1)} copy(bf16[32,8,256]{2,1,0:T(8,128)(2,1)} %shard_map.37) | data formatting | bytes 262144

commit v3 on v2

v3 whole, which is shorter than its diff:
```python
import functools

import jax
import jax.numpy as jnp
from jax import lax
from jax.experimental import pallas as pl
from jax.experimental.pallas import tpu as pltpu
from jax.sharding import PartitionSpec as P

SLOTS = 8
LAG = 12
LANES = 128
MESH = pl.DeviceIdType.MESH


def kernel(n, q_hbm, k_hbm, v_hbm, out, q, k, v, raw, weights, halves, seen, stats, seen_in, stats_in, merged, merged_stats, q_sem, k_sem, v_sem, send_sem, recv_sem, out_sem):
    me = lax.axis_index("sp")
    chip, core = me // 2, me % 2
    chips = n // 2
    heads, head = q.shape[1:]
    rows = k.shape[1] * heads

    def owner(step):
        if isinstance(step, int) and step >= n - 2:
            return me if step == n - 1 else lax.bitwise_xor(me, 1)
        second = step // (chips - 1)
        other = lax.bitwise_xor(chip, (chips - 1) * (1 + second) - step) * 2 + second
        return other if isinstance(step, int) else jnp.where(step < n - 2, other, jnp.where(step == n - 2, lax.bitwise_xor(me, 1), me))

    def load(hbm, buf, sem, step):
        slot = lax.rem(step, SLOTS)
        return pltpu.make_async_copy(hbm.at[owner(step)], buf.at[slot], sem.at[slot])

    def start(hbm, buf, sem, step):
        load(hbm, buf, sem, step).start()

    def wait(hbm, buf, sem, step):
        load(hbm, buf, sem, step).wait()

    keys, vals = (k_hbm, k, k_sem), (v_hbm, v, v_sem)
    q_copy = pltpu.make_async_copy(q_hbm, q, q_sem)
    q_copy.start()

    @pl.loop(0, SLOTS)
    def _(step):
        start(*keys, step)
        start(*vals, step)

    barrier = pltpu.get_barrier_semaphore()

    @pl.loop(1, n)
    def _(hop):
        pl.semaphore_signal(barrier, inc=1, device_id={"sp": lax.rem(me + hop, n)}, device_id_type=MESH)

    q_copy.wait()
    lane = lax.broadcasted_iota(jnp.int32, (heads, rows), 1)
    own = lane % heads == lax.broadcasted_iota(jnp.int32, (heads, rows), 0)

    def scores(step):
        block = k[lax.rem(step, SLOTS)].reshape(rows, head)
        return lax.dot_general(q[owner(step)], block, (((1,), (1,)), ((), ())), preferred_element_type=jnp.float32)

    def soften(step, s):
        s = jnp.where(own, s * head**-0.5, -jnp.inf)
        high = jnp.max(s, -1, keepdims=True)
        w = jnp.exp(s - high)
        stats[step, :, :LANES] = jnp.broadcast_to(high, (heads, LANES))
        stats[step, :, LANES:] = jnp.broadcast_to(jnp.sum(w, -1, keepdims=True), (heads, LANES))
        return w.astype(jnp.bfloat16)

    def dot(w, block):
        return lax.dot_general(w, block, (((1,), (0,)), ((), ())), preferred_element_type=jnp.float32)

    def values(step, w):
        block = v[lax.rem(step, SLOTS)].reshape(rows, head)
        half = rows // 2
        return dot(w[:, :half], block[:half]) + dot(w[:, half:], block[half:])

    def values_apart(step, w):
        half = v.shape[1] // 2
        for i in range(2):
            halves[i] = dot(w[:, i * rows // 2 : (i + 1) * rows // 2], v[step % SLOTS, i * half : (i + 1) * half].reshape(rows // 2, head))
        return halves[0] + halves[1]

    def send(step):
        to = owner(step)
        slot, group = lax.bitwise_xor(me, to), step // (n - 2)
        for i, (src, dst) in enumerate(((seen, seen_in), (stats, stats_in))):
            pltpu.make_async_remote_copy(
                src.at[step], dst.at[slot], send_sem.at[i], recv_sem.at[group, i], device_id={"sp": to}, device_id_type=MESH
            ).start()

    def put(step, o):
        seen[step] = o.astype(jnp.bfloat16)

    wait(*keys, 0)
    raw[...] = scores(0)
    start(*keys, SLOTS)
    wait(*keys, 1)
    old = raw[...]
    raw[...] = scores(1)
    weights[...] = soften(0, old)
    start(*keys, SLOTS + 1)

    @pl.loop(2, n)
    def _(step):
        wait(*vals, step - 2)
        wait(*keys, step)
        old, w = raw[...], weights[...]
        new = scores(step)
        o = values(step - 2, w)
        weights[...] = soften(step - 1, old)
        raw[...] = new
        put(step - 2, o)

        @pl.when(step - 2 + SLOTS < n)
        def _():
            start(*vals, step - 2 + SLOTS)

        @pl.when(step + SLOTS < n)
        def _():
            start(*keys, step + SLOTS)

        @pl.when(step == LAG)
        def _():
            pl.semaphore_wait(barrier, n - 1)

            @pl.loop(0, LAG - 2)
            def _(earlier):
                send(earlier)

        @pl.when(step >= LAG)
        def _():
            send(step - 2)

    def merge():
        for i, ref in enumerate((seen_in, stats_in)):
            pltpu.make_async_copy(ref.at[pl.ds(2, n - 2)], ref.at[pl.ds(2, n - 2)], recv_sem.at[0, i]).wait()
        top = tree(jnp.maximum, [stats_in[i, :, :LANES] for i in range(2, n)])
        bottoms, uppers = [], []
        for i in range(2, n):
            scale = jnp.exp(stats_in[i, :, :LANES] - top)
            bottoms.append(scale * stats_in[i, :, LANES:])
            uppers.append(wide(scale) * seen_in[i].astype(jnp.float32))
        merged_stats[:, :LANES] = top
        merged_stats[:, LANES:] = tree(jnp.add, bottoms)
        merged[...] = tree(jnp.add, uppers)

    def tree(op, items):
        while len(items) > 1:
            items = [op(*items[i : i + 2]) if i + 1 < len(items) else items[i] for i in range(0, len(items), 2)]
        return items[0]

    def wide(x):
        return jnp.concatenate([x] * (head // LANES), -1)

    before = weights[...]
    w = soften(n - 1, raw[...])
    wait(*vals, n - 2)
    put(n - 2, values(n - 2, before))
    send(n - 2)

    @pl.when(core == 0)
    def _():
        merge()

    wait(*vals, n - 1)
    halves[0] = values_apart(n - 1, w)

    @pl.when(core == 1)
    def _():
        merge()

    for i, ref in enumerate((seen_in, stats_in)):
        pltpu.make_async_copy(ref.at[1], ref.at[1], recv_sem.at[1, i]).wait()
    highs = [stats[n - 1, :, :LANES], stats_in[1, :, :LANES], merged_stats[:, :LANES]]
    totals = [stats[n - 1, :, LANES:], stats_in[1, :, LANES:], merged_stats[:, LANES:]]
    parts = [halves[0], seen_in[1].astype(jnp.float32), merged[...]]
    top = tree(jnp.maximum, highs)
    scales = [jnp.exp(x - top) for x in highs]
    bottom = tree(jnp.add, [x * y for x, y in zip(scales, totals)])
    upper = tree(jnp.add, [wide(x) * y for x, y in zip(scales, parts)])
    out[me] = (upper / wide(bottom)).astype(jnp.bfloat16)

    @pl.loop(0, n - 1)
    def _(i):
        to = i + (i >= me).astype(jnp.int32)
        pltpu.make_async_remote_copy(out.at[me], out.at[me], out_sem.at[0], out_sem.at[1], device_id={"sp": to}, device_id_type=MESH).start()

    for ref, sem in ((seen, send_sem.at[0]), (stats, send_sem.at[1]), (out, out_sem.at[0]), (out, out_sem.at[1])):
        pltpu.make_async_copy(ref.at[pl.ds(0, n - 1)], ref.at[pl.ds(0, n - 1)], sem).wait()


def solution(mesh):
    n = mesh.shape["sp"]

    def step(q, k, v):
        seqs, tokens, heads, head = k.shape
        assert seqs == n
        return pl.pallas_call(
            functools.partial(kernel, n),
            out_shape=pltpu.VMEM(q.shape, q.dtype),
            in_specs=[pl.BlockSpec(memory_space=pltpu.HBM)] * 3,
            out_specs=pl.BlockSpec(memory_space=pltpu.VMEM),
            scratch_shapes=[
                pltpu.VMEM(q.shape, q.dtype),
                pltpu.VMEM((SLOTS, tokens, heads, head), k.dtype),
                pltpu.VMEM((SLOTS, tokens, heads, head), v.dtype),
                pltpu.VMEM((heads, tokens * heads), jnp.float32),
                pltpu.VMEM((heads, tokens * heads), jnp.bfloat16),
                pltpu.VMEM((2, heads, head), jnp.float32),
                pltpu.VMEM((n, heads, head), jnp.bfloat16),
                pltpu.VMEM((n, heads, 2 * LANES), jnp.float32),
                pltpu.VMEM((n, heads, head), jnp.bfloat16),
                pltpu.VMEM((n, heads, 2 * LANES), jnp.float32),
                pltpu.VMEM((heads, head), jnp.float32),
                pltpu.VMEM((heads, 2 * LANES), jnp.float32),
                pltpu.SemaphoreType.DMA,
                pltpu.SemaphoreType.DMA((SLOTS,)),
                pltpu.SemaphoreType.DMA((SLOTS,)),
                pltpu.SemaphoreType.DMA((2,)),
                pltpu.SemaphoreType.DMA((2, 2)),
                pltpu.SemaphoreType.DMA((2,)),
            ],
            compiler_params=pltpu.CompilerParams(collective_id=0, has_side_effects=True, vmem_limit_bytes=67043328 - 192 * 1024),
        )(q, k, v)

    return jax.shard_map(
        step,
        mesh=mesh,
        in_specs=(P("dp", None, None), P("dp", "sp", None, None), P("dp", "sp", None, None)),
        out_specs=P("dp", None, None),
        check_vma=False,
    )
```

time: 34.4 us -> 31.9 us (0.927)
  Pallas kernels: 32.6 us -> 31.1 us
  local copies, waits for them, and re-layouts: 1.57 us -> 0.66 us
    pallas_call x1, Pallas kernels: 32.6 us -> 31.1 us  [step(): pl.pallas_call(functools.partial(kernel, n), out_shape=pltpu.VMEM(q.shape...]
    unnamed x1, local copies, waits for them, and re-layouts: 1.57 us -> 0.66 us
where the time goes in v3:
time: 31.9 us; the launch traced here: 31.7 us
  Pallas kernels  31.1 us (97%)
  local copies, waits for them, and re-layouts  0.66 us (2%)
    pallas_call x1, Pallas kernels, step(): pl.pallas_call(functools.partial(kernel, n), out_shape=pltpu.VMEM(q.shape...  31.1 us
    unnamed x1, local copies, waits for them, and re-layouts  0.66 us

profile of v3, /device:TPU:0, one launch (start us, length us, event | category | flops | bytes accessed | tf_op | source)
XLA Modules:
  0.0 31.7 jit_solution(11012951115900917227)
XLA Ops:
  0.0 31.1 %shard_map.37 = bf16[32,8,256]{2,1,0:T(8,128)(2,1)S(1)} custom-call(bf16[32,8,256]{2,1,0:T(8,128)(2,1)} %q_hbm.1, bf16[32,256,8,256]{3,2,1,0:T(8,128)(2,1)} %k_hbm.1, bf16[32,256,8,256]{3,2,1,0:T(8,128)(2,1)} %v_hbm.1), custom_call_target="tpu_custom_call" | custom-call | tf_op jit(solution)/shard_map/pallas_call | solution.py:200
  31.1 0.7 %copy.5 = bf16[32,8,256]{2,1,0:T(8,128)(2,1)} copy(bf16[32,8,256]{2,1,0:T(8,128)(2,1)S(1)} %shard_map.37) | data formatting | bytes 262144

commit v4 on v3

--- a/solution.py
+++ b/solution.py
@@ -13,7 +13,7 @@
 MESH = pl.DeviceIdType.MESH
 
 
-def kernel(n, q_hbm, k_hbm, v_hbm, out, q, k, v, raw, weights, halves, seen, stats, seen_in, stats_in, merged, merged_stats, q_sem, k_sem, v_sem, send_sem, recv_sem, out_sem):
+def kernel(n, q_hbm, k_hbm, v_hbm, out, q, k, v, raw, weights, halves, last, seen, stats, seen_in, stats_in, merged, merged_stats, q_sem, k_sem, v_sem, send_sem, recv_sem, out_sem):
     me = lax.axis_index("sp")
     chip, core = me // 2, me % 2
     chips = n // 2
@@ -92,46 +92,6 @@
 
     def put(step, o):
         seen[step] = o.astype(jnp.bfloat16)
-
-    wait(*keys, 0)
-    raw[...] = scores(0)
-    start(*keys, SLOTS)
-    wait(*keys, 1)
-    old = raw[...]
-    raw[...] = scores(1)
-    weights[...] = soften(0, old)
-    start(*keys, SLOTS + 1)
-
-    @pl.loop(2, n)
-    def _(step):
-        wait(*vals, step - 2)
-        wait(*keys, step)
-        old, w = raw[...], weights[...]
-        new = scores(step)
-        o = values(step - 2, w)
-        weights[...] = soften(step - 1, old)
-        raw[...] = new
-        put(step - 2, o)
-
-        @pl.when(step - 2 + SLOTS < n)
-        def _():
-            start(*vals, step - 2 + SLOTS)
-
-        @pl.when(step + SLOTS < n)
-        def _():
-            start(*keys, step + SLOTS)
-
-        @pl.when(step == LAG)
-        def _():
-            pl.semaphore_wait(barrier, n - 1)
-
-            @pl.loop(0, LAG - 2)
-            def _(earlier):
-                send(earlier)
-
-        @pl.when(step >= LAG)
-        def _():
-            send(step - 2)
 
     def merge():
         for i, ref in enumerate((seen_in, stats_in)):
@@ -154,18 +114,97 @@
     def wide(x):
         return jnp.concatenate([x] * (head // LANES), -1)
 
-    before = weights[...]
-    w = soften(n - 1, raw[...])
-    wait(*vals, n - 2)
-    put(n - 2, values(n - 2, before))
-    send(n - 2)
-
-    @pl.when(core == 0)
-    def _():
-        merge()
-
-    wait(*vals, n - 1)
-    halves[0] = values_apart(n - 1, w)
+    wait(*keys, 0)
+    raw[...] = scores(0)
+    start(*keys, SLOTS)
+    wait(*keys, 1)
+    old = raw[...]
+    raw[...] = scores(1)
+    weights[...] = soften(0, old)
+    start(*keys, SLOTS + 1)
+
+    @pl.loop(2, n - 2)
+    def _(step):
+        wait(*vals, step - 2)
+        wait(*keys, step)
+        old, w = raw[...], weights[...]
+        new = scores(step)
+        o = values(step - 2, w)
+        weights[...] = soften(step - 1, old)
+        raw[...] = new
+        put(step - 2, o)
+
+        @pl.when(step - 2 + SLOTS < n)
+        def _():
+            start(*vals, step - 2 + SLOTS)
+
+        @pl.when(step + SLOTS < n - 2)
+        def _():
+            start(*keys, step + SLOTS)
+
+        @pl.when(step - 2 + SLOTS == n - 3)
+        def _():
+            start(*keys, n - 2)
+            start(*keys, n - 1)
+
+        @pl.when(step == LAG)
+        def _():
+            pl.semaphore_wait(barrier, n - 1)
+
+            @pl.loop(0, LAG - 2)
+            def _(earlier):
+                send(earlier)
+
+        @pl.when(step >= LAG)
+        def _():
+            send(step - 2)
+
+        @pl.when((step == n - 6) & (core == 0))
+        def _():
+            merge()
+
+    def block(f):
+        @pl.loop(0, 1 + me // n)
+        def _(_):
+            f()
+
+    @block
+    def _():
+        w = soften(n - 3, raw[...])
+        wait(*vals, n - 4)
+        put(n - 4, values_apart(n - 4, weights[...]))
+        weights[...] = w
+        send(n - 4)
+
+    @block
+    def _():
+        wait(*vals, n - 3)
+        put(n - 3, values_apart(n - 3, weights[...]))
+        send(n - 3)
+
+    @block
+    def _():
+        wait(*keys, n - 2)
+        raw[...] = scores(n - 2)
+
+    @block
+    def _():
+        wait(*keys, n - 1)
+        old = raw[...]
+        raw[...] = scores(n - 1)
+        weights[...] = soften(n - 2, old)
+
+    @block
+    def _():
+        wait(*vals, n - 2)
+        put(n - 2, values_apart(n - 2, weights[...]))
+        weights[...] = soften(n - 1, raw[...])
+        send(n - 2)
+
+    @block
+    def _():
+        wait(*vals, n - 1)
+        last[...] = values_apart(n - 1, weights[...])
 
     @pl.when(core == 1)
     def _():
@@ -175,7 +214,7 @@
         pltpu.make_async_copy(ref.at[1], ref.at[1], recv_sem.at[1, i]).wait()
     highs = [stats[n - 1, :, :LANES], stats_in[1, :, :LANES], merged_stats[:, :LANES]]
     totals = [stats[n - 1, :, LANES:], stats_in[1, :, LANES:], merged_stats[:, LANES:]]
-    parts = [halves[0], seen_in[1].astype(jnp.float32), merged[...]]
+    parts = [last[...], seen_in[1].astype(jnp.float32), merged[...]]
     top = tree(jnp.maximum, highs)
     scales = [jnp.exp(x - top) for x in highs]
     bottom = tree(jnp.add, [x * y for x, y in zip(scales, totals)])
@@ -209,6 +248,7 @@
                 pltpu.VMEM((heads, tokens * heads), jnp.float32),
                 pltpu.VMEM((heads, tokens * heads), jnp.bfloat16),
                 pltpu.VMEM((2, heads, head), jnp.float32),
+                pltpu.VMEM((heads, head), jnp.float32),
                 pltpu.VMEM((n, heads, head), jnp.bfloat16),
                 pltpu.VMEM((n, heads, 2 * LANES), jnp.float32),
                 pltpu.VMEM((n, heads, head), jnp.bfloat16),

time: 31.9 us -> 31.5 us (0.987)
  Pallas kernels: 31.1 us -> 30.7 us
    pallas_call x1, Pallas kernels: 31.1 us -> 30.7 us  [step(): pl.pallas_call(functools.partial(kernel, n), out_shape=pltpu.VMEM(q.shape...]
where the time goes in v4:
time: 31.5 us; the launch traced here: 31.4 us
  Pallas kernels  30.7 us (97%)
  local copies, waits for them, and re-layouts  0.66 us (2%)
    pallas_call x1, Pallas kernels, step(): pl.pallas_call(functools.partial(kernel, n), out_shape=pltpu.VMEM(q.shape...  30.7 us
    unnamed x1, local copies, waits for them, and re-layouts  0.66 us

profile of v4, /device:TPU:0, one launch (start us, length us, event | category | flops | bytes accessed | tf_op | source)
XLA Modules:
  0.0 31.4 jit_solution(537338766083808520)
XLA Ops:
  0.0 30.7 %shard_map.37 = bf16[32,8,256]{2,1,0:T(8,128)(2,1)S(1)} custom-call(bf16[32,8,256]{2,1,0:T(8,128)(2,1)} %q_hbm.1, bf16[32,256,8,256]{3,2,1,0:T(8,128)(2,1)} %k_hbm.1, bf16[32,256,8,256]{3,2,1,0:T(8,128)(2,1)} %v_hbm.1), custom_call_target="tpu_custom_call" | custom-call | tf_op jit(solution)/shard_map/pallas_call | solution.py:239
  30.7 0.7 %copy.5 = bf16[32,8,256]{2,1,0:T(8,128)(2,1)} copy(bf16[32,8,256]{2,1,0:T(8,128)(2,1)S(1)} %shard_map.37) | data formatting | bytes 262144

commit v5 on v4

v5 whole, which is shorter than its diff:
```python
import functools

import jax
import jax.numpy as jnp
from jax import lax
from jax.experimental import pallas as pl
from jax.experimental.pallas import tpu as pltpu
from jax.sharding import PartitionSpec as P

SLOTS = 8
LAG = 13
BEHIND = 4
LANES = 128
MESH = pl.DeviceIdType.MESH


def kernel(n, q_hbm, k_hbm, v_hbm, out, q, k, v, raw, weights, halves, last, seen, stats, seen_in, stats_in, merged, merged_stats, q_sem, k_sem, v_sem, send_sem, recv_sem, out_sem):
    me = lax.axis_index("sp")
    chip, core = me // 2, me % 2
    chips = n // 2
    heads, head = q.shape[1:]
    rows = k.shape[1] * heads

    near, far = chip == 0, chip == chips - 1

    def work(step):
        step = jnp.asarray(step, jnp.int32)
        last_two, skips = step - (n - 2), jnp.where(near, 0, 1)
        turn = step - jnp.where(far, 0, 2)
        second = (turn >= chips - 1 - skips).astype(jnp.int32)
        mask = chips - 1 - (turn - second * (chips - 1 - skips))
        mask = mask - jnp.where(near, 0, (mask <= chip).astype(jnp.int32))
        to_far = chips - 1 - chip
        swaps = jnp.logical_not(far) & (to_far < 4)
        mask = jnp.where(swaps & (mask == chips - 1), to_far, jnp.where(swaps & (mask == to_far), chips - 1, mask))
        seq = lax.bitwise_xor(chip, mask) * 2 + second
        seq = jnp.where((last_two >= 0) & jnp.logical_not(near), lax.bitwise_xor(me, 1 - last_two), seq)
        end = lax.bitwise_xor(me, (step < n - 2).astype(jnp.int32)) - jnp.where((step == n - 3) | (step == n - 2), n - 2, 0)
        return jnp.where(far & (step >= n - 4), end, jnp.where(jnp.logical_not(far) & (step < 2), step, seq))

    early = (core == 0) & jnp.logical_not(near)

    def owner(seq):
        return seq + jnp.where(seq < 2, n - 2, 0)

    def load(hbm, buf, sem, step):
        slot = lax.rem(step, SLOTS)
        return pltpu.make_async_copy(hbm.at[work(step)], buf.at[slot], sem.at[slot])

    def start(hbm, buf, sem, step):
        load(hbm, buf, sem, step).start()

    def wait(hbm, buf, sem, step):
        load(hbm, buf, sem, step).wait()

    keys, vals = (k_hbm, k, k_sem), (v_hbm, v, v_sem)
    q_copy = pltpu.make_async_copy(q_hbm, q, q_sem)
    q_copy.start()

    @pl.loop(0, BEHIND)
    def _(step):
        start(*keys, step)

    @pl.loop(0, SLOTS)
    def _(step):
        start(*vals, step)

        @pl.when(step + BEHIND < SLOTS)
        def _():
            start(*keys, step + BEHIND)

    barrier = pltpu.get_barrier_semaphore()

    @pl.loop(1, n)
    def _(hop):
        pl.semaphore_signal(barrier, inc=1, device_id={"sp": lax.rem(me + hop, n)}, device_id_type=MESH)

    q_copy.wait()
    lane = lax.broadcasted_iota(jnp.int32, (heads, rows), 1)
    own = lane % heads == lax.broadcasted_iota(jnp.int32, (heads, rows), 0)

    def scores(step):
        block = k[lax.rem(step, SLOTS)].reshape(rows, head)
        return lax.dot_general(q[work(step)], block, (((1,), (1,)), ((), ())), preferred_element_type=jnp.float32)

    def soften(step, s):
        s = jnp.where(own, s * head**-0.5, -jnp.inf)
        high = jnp.max(s, -1, keepdims=True)
        w = jnp.exp(s - high)
        stats[step, :, :LANES] = jnp.broadcast_to(high, (heads, LANES))
        stats[step, :, LANES:] = jnp.broadcast_to(jnp.sum(w, -1, keepdims=True), (heads, LANES))
        return w.astype(jnp.bfloat16)

    def dot(w, block):
        return lax.dot_general(w, block, (((1,), (0,)), ((), ())), preferred_element_type=jnp.float32)

    def values(step, w):
        block = v[lax.rem(step, SLOTS)].reshape(rows, head)
        half = rows // 2
        return dot(w[:, :half], block[:half]) + dot(w[:, half:], block[half:])

    def values_apart(i, step, w):
        half = v.shape[1] // 2
        for part in range(2):
            halves[i, part] = dot(w[:, part * rows // 2 : (part + 1) * rows // 2], v[step % SLOTS, part * half : (part + 1) * half].reshape(rows // 2, head))
        return halves[i, 0] + halves[i, 1]

    def send(step):
        seq = work(step)
        to = owner(seq)
        which = lax.bitwise_xor(me, to)
        extra = (seq < 2).astype(jnp.int32)

        @pl.when(which > 0)
        def _():
            for i, (src, dst) in enumerate(((seen, seen_in), (stats, stats_in))):
                pltpu.make_async_remote_copy(
                    src.at[step],
                    dst.at[extra, which],
                    send_sem.at[i],
                    recv_sem.at[extra, (which == 1).astype(jnp.int32), i],
                    device_id={"sp": to},
                    device_id_type=MESH,
                ).start()

    def put(step, o):
        seen[step] = o.astype(jnp.bfloat16)

    def merge(extra):
        for i, ref in enumerate((seen_in, stats_in)):
            pltpu.make_async_copy(ref.at[extra, pl.ds(2, n - 2)], ref.at[extra, pl.ds(2, n - 2)], recv_sem.at[extra, 0, i]).wait()
        top = tree(jnp.maximum, [stats_in[extra, i, :, :LANES] for i in range(2, n)])
        bottoms, uppers = [], []
        for i in range(2, n):
            scale = jnp.exp(stats_in[extra, i, :, :LANES] - top)
            bottoms.append(scale * stats_in[extra, i, :, LANES:])
            uppers.append(wide(scale) * seen_in[extra, i].astype(jnp.float32))
        merged_stats[extra, :, :LANES] = top
        merged_stats[extra, :, LANES:] = tree(jnp.add, bottoms)
        merged[extra] = tree(jnp.add, uppers)

    def tree(op, items):
        while len(items) > 1:
            items = [op(*items[i : i + 2]) if i + 1 < len(items) else items[i] for i in range(0, len(items), 2)]
        return items[0]

    def wide(x):
        return jnp.concatenate([x] * (head // LANES), -1)

    def keep(step, w):
        weights[lax.rem(step, BEHIND)] = w

    @pl.loop(0, BEHIND)
    def _(step):
        wait(*keys, step)
        old = raw[...]
        raw[...] = scores(step)

        @pl.when(step > 0)
        def _():
            keep(step - 1, soften(step - 1, old))

        start(*keys, step + SLOTS)

    @pl.loop(BEHIND, n)
    def _(step):
        wait(*vals, step - BEHIND)
        wait(*keys, step)
        old, w = raw[...], weights[lax.rem(step, BEHIND)]
        new = scores(step)
        o = values(step - BEHIND, w)
        keep(step - 1, soften(step - 1, old))
        raw[...] = new
        put(step - BEHIND, o)

        @pl.when(step - BEHIND + SLOTS < n)
        def _():
            start(*vals, step - BEHIND + SLOTS)

        @pl.when(step + SLOTS < n)
        def _():
            start(*keys, step + SLOTS)

        @pl.when(step == LAG)
        def _():
            pl.semaphore_wait(barrier, n - 1)

            @pl.loop(0, LAG - BEHIND)
            def _(earlier):
                send(earlier)

        @pl.when(step >= LAG)
        def _():
            send(step - BEHIND)

        @pl.when((step == n - 4) & far)
        def _():
            merge(1)

        @pl.when((step == n - 4) & early)
        def _():
            merge(0)

    def block(f):
        @pl.loop(0, 1 + me // n)
        def _(_):
            f()

    def finish(step):
        wait(*vals, step)
        o = values_apart(0, step, weights[step % BEHIND])
        put(step, o)
        if step >= n - 2:
            last[n - 1 - step] = o
        send(step)

    @block
    def _():
        keep(n - 1, soften(n - 1, raw[...]))
        finish(n - BEHIND)

    for step in range(n - BEHIND + 1, n):
        block(functools.partial(finish, step))

    @pl.when((core == 1) & jnp.logical_not(near))
    def _():
        merge(0)

    def combine(extra, seq):
        for i, ref in enumerate((seen_in, stats_in)):
            pltpu.make_async_copy(ref.at[extra, 1], ref.at[extra, 1], recv_sem.at[extra, 1, i]).wait()
        mine = stats[n - 1 - extra]
        both = [mine, stats_in[extra, 1], merged_stats[extra]]
        highs, totals = [x[:, :LANES] for x in both], [x[:, LANES:] for x in both]
        parts = [last[extra], seen_in[extra, 1].astype(jnp.float32), merged[extra]]
        top = tree(jnp.maximum, highs)
        scales = [jnp.exp(x - top) for x in highs]
        bottom = tree(jnp.add, [x * y for x, y in zip(scales, totals)])
        upper = tree(jnp.add, [wide(x) * y for x, y in zip(scales, parts)])
        out[seq] = (upper / wide(bottom)).astype(jnp.bfloat16)

    def share(seq, to):
        pltpu.make_async_remote_copy(out.at[seq], out.at[seq], out_sem.at[0], out_sem.at[1], device_id={"sp": to}, device_id_type=MESH).start()

    @pl.when(far)
    def _():
        combine(1, core)
        share(core, 0)
        share(core, 1)

    @pl.when(jnp.logical_not(near))
    def _():
        combine(0, me)
        share(me, 0)
        share(me, 1)

        @pl.loop(1, n)
        def _(i):
            to = lax.bitwise_xor(me, n - i)

            @pl.when(to >= 2)
            def _():
                share(me, to)

                @pl.when(far)
                def _():
                    share(core, to)

    middle = jnp.logical_not(near | far)

    def ended(ref, sem, *counts):
        for chips_of, count in zip((near, far, middle), counts):
            if count:
                block = ref.at[pl.ds(0, count)] if count <= n else seen_in.at[:, pl.ds(0, count // 2)]
                pl.when(chips_of)(pltpu.make_async_copy(block, block, sem).wait)

    ended(seen, send_sem.at[0], n, n - 2, n - 1)
    ended(stats, send_sem.at[1], n, n - 2, n - 1)
    ended(out, out_sem.at[0], 0, 2 * n - 2, n - 1)
    ended(out, out_sem.at[1], n, n - 2, n - 1)


def solution(mesh):
    n = mesh.shape["sp"]

    def step(q, k, v):
        seqs, tokens, heads, head = k.shape
        assert seqs == n
        return pl.pallas_call(
            functools.partial(kernel, n),
            out_shape=pltpu.VMEM(q.shape, q.dtype),
            in_specs=[pl.BlockSpec(memory_space=pltpu.HBM)] * 3,
            out_specs=pl.BlockSpec(memory_space=pltpu.VMEM),
            scratch_shapes=[
                pltpu.VMEM(q.shape, q.dtype),
                pltpu.VMEM((SLOTS, tokens, heads, head), k.dtype),
                pltpu.VMEM((SLOTS, tokens, heads, head), v.dtype),
                pltpu.VMEM((heads, tokens * heads), jnp.float32),
                pltpu.VMEM((BEHIND, heads, tokens * heads), jnp.bfloat16),
                pltpu.VMEM((2, 2, heads, head), jnp.float32),
                pltpu.VMEM((2, heads, head), jnp.float32),
                pltpu.VMEM((n, heads, head), jnp.bfloat16),
                pltpu.VMEM((n, heads, 2 * LANES), jnp.float32),
                pltpu.VMEM((2, n, heads, head), jnp.bfloat16),
                pltpu.VMEM((2, n, heads, 2 * LANES), jnp.float32),
                pltpu.VMEM((2, heads, head), jnp.float32),
                pltpu.VMEM((2, heads, 2 * LANES), jnp.float32),
                pltpu.SemaphoreType.DMA,
                pltpu.SemaphoreType.DMA((SLOTS,)),
                pltpu.SemaphoreType.DMA((SLOTS,)),
                pltpu.SemaphoreType.DMA((2,)),
                pltpu.SemaphoreType.DMA((2, 2, 2)),
                pltpu.SemaphoreType.DMA((2,)),
            ],
            compiler_params=pltpu.CompilerParams(collective_id=0, has_side_effects=True, vmem_limit_bytes=67043328 - 192 * 1024),
        )(q, k, v)

    return jax.shard_map(
        step,
        mesh=mesh,
        in_specs=(P("dp", None, None), P("dp", "sp", None, None), P("dp", "sp", None, None)),
        out_specs=P("dp", None, None),
        check_vma=False,
    )
```

time: 31.5 us -> 31.4 us (level)
  no operation moved by 1% of the time
where the time goes in v5:
time: 31.4 us; the launch traced here: 31.2 us
  Pallas kernels  30.5 us (97%)
  local copies, waits for them, and re-layouts  0.66 us (2%)
    pallas_call x1, Pallas kernels, step(): pl.pallas_call(functools.partial(kernel, n), out_shape=pltpu.VMEM(q.shape...  30.5 us
    unnamed x1, local copies, waits for them, and re-layouts  0.66 us

profile of v5, /device:TPU:0, one launch (start us, length us, event | category | flops | bytes accessed | tf_op | source)
XLA Modules:
  0.0 31.2 jit_solution(6535721017821944254)
XLA Ops:
  0.0 30.5 %shard_map.37 = bf16[32,8,256]{2,1,0:T(8,128)(2,1)S(1)} custom-call(bf16[32,8,256]{2,1,0:T(8,128)(2,1)} %q_hbm.1, bf16[32,256,8,256]{3,2,1,0:T(8,128)(2,1)} %k_hbm.1, bf16[32,256,8,256]{3,2,1,0:T(8,128)(2,1)} %v_hbm.1), custom_call_target="tpu_custom_call" | custom-call | tf_op jit(solution)/shard_map/pallas_call | solution.py:289
  30.6 0.7 %copy.5 = bf16[32,8,256]{2,1,0:T(8,128)(2,1)} copy(bf16[32,8,256]{2,1,0:T(8,128)(2,1)S(1)} %shard_map.37) | data formatting | bytes 262144

commit v6 on v5

--- a/solution.py
+++ b/solution.py
@@ -254,11 +254,11 @@
         share(me, 0)
         share(me, 1)
 
-        @pl.loop(1, n)
+        @pl.loop(0, n)
         def _(i):
-            to = lax.bitwise_xor(me, n - i)
-
-            @pl.when(to >= 2)
+            to = lax.bitwise_xor(me, jnp.where(far, n - 1 - i, lax.rem(i + n // 4, n)))
+
+            @pl.when((to >= 2) & (to != me))
             def _():
                 share(me, to)
 

time: 31.4 us -> 31.2 us (level)
  no operation moved by 1% of the time
where the time goes in v6:
time: 31.2 us; the launch traced here: 31.1 us
  Pallas kernels  30.4 us (97%)
  local copies, waits for them, and re-layouts  0.66 us (2%)
    pallas_call x1, Pallas kernels, step(): pl.pallas_call(functools.partial(kernel, n), out_shape=pltpu.VMEM(q.shape...  30.4 us
    unnamed x1, local copies, waits for them, and re-layouts  0.66 us

profile of v6, /device:TPU:0, one launch (start us, length us, event | category | flops | bytes accessed | tf_op | source)
XLA Modules:
  0.0 31.1 jit_solution(2479647323361182494)
XLA Ops:
  0.0 30.4 %shard_map.37 = bf16[32,8,256]{2,1,0:T(8,128)(2,1)S(1)} custom-call(bf16[32,8,256]{2,1,0:T(8,128)(2,1)} %q_hbm.1, bf16[32,256,8,256]{3,2,1,0:T(8,128)(2,1)} %k_hbm.1, bf16[32,256,8,256]{3,2,1,0:T(8,128)(2,1)} %v_hbm.1), custom_call_target="tpu_custom_call" | custom-call | tf_op jit(solution)/shard_map/pallas_call | solution.py:289
  30.4 0.7 %copy.5 = bf16[32,8,256]{2,1,0:T(8,128)(2,1)} copy(bf16[32,8,256]{2,1,0:T(8,128)(2,1)S(1)} %shard_map.37) | data formatting | bytes 262144
